TPU v7x, 512 devices: a whole 4x8x8 slice. The times are simulated.
512 devices in a mesh: seq: 32 (over x, y), chan: 8 (over z), dp: 2 (over core).
Axes of the slice: x: 4, y: 8, z: 8, core: 2. Of those that a mesh axis runs over, the one named last changes fastest.
Arguments:
- ssm_input: bfloat16 [2, 4096, 4096], P('dp', 'seq', 'chan'), may hold values from -6 to 6
- gate_z: bfloat16 [2, 4096, 4096], P('dp', 'seq', 'chan'), may hold values from -6 to 6
- b_proj: bfloat16 [2, 4096, 128], P('dp', 'seq'), may hold values from -0.52734375 to 0.52734375
- c_proj: bfloat16 [2, 4096, 128], P('dp', 'seq'), may hold values from -6 to 6
- step_size: float32 [2, 4096, 64], P('dp', 'seq', 'chan'), may hold values from 0.02 to 0.2
- log_decay: float32 [2, 4096, 64], P('dp', 'seq', 'chan'), may hold values from -1 to 0, as said below
- skip_d: float32 [64], P('chan'), may hold values from 0.5 to 1.5
- norm_gain: float32 [4096], P('chan'), may hold values from 0.5 to 1.5
- w_out: bfloat16 [4096, 2048], P('chan'), may hold values from -0.09375 to 0.09375
- d_out: bfloat16 [2, 4096, 2048], P('dp', 'seq', 'chan'), may hold values from -6 to 6
- game_lengths: int32 [2, 4], P('dp'), may hold values from 1 to 2048, 4096 in all within a row
Outputs:
- out: bfloat16 [2, 4096, 2048], P('dp', 'seq', 'chan')
- grad_x: bfloat16 [2, 4096, 4096], P('dp', 'seq', 'chan')
- grad_gain: float32 [4096], P('chan')
- grad_skip: float32 [64], P('chan')
Inputs may be any that keep to these rules, and one draw needn't show every extreme that they name: `game_lengths`: each row's 4 game lengths sum to 4096, and the longest is exactly 2048. `log_decay`: a log decay per position and head.
All inputs are finite; a program needn't handle non-finite values.
Results may differ from a plain program's by a relative error of at most 0.017.
Values may be sent and summed in bfloat16 or wider, within the bound.
A program may use at most 64 MiB of HBM per device.

v0:
```python
import jax
import jax.numpy as jnp
from jax import lax
from jax.sharding import Mesh
from jax.sharding import PartitionSpec as P

SEQ = ("seq_0", "seq_1")
SEQ_DP = ("seq_0", "seq_1", "dp")


NORM_EPS = 1e-05


def filled_with(value, identity):
    return jax.tree.map(
        lambda part, zero: jnp.zeros_like(part) + jnp.asarray(zero, part.dtype), value, identity
    )


def prefix_by_axis(value, axes, combine, identity, reverse):
    before = start = filled_with(value, identity)
    so_far = value
    for axis in reversed(axes):
        length, mine = (lax.axis_size(axis), lax.axis_index(axis))
        pieces = jax.tree.map(
            lambda part, kind: lax.all_gather(part.astype(kind), axis),
            so_far,
            (jnp.bfloat16, jnp.bfloat16),
        )
        inside, so_far = (start, start)
        for k in reversed(range(length)) if reverse else range(length):
            passed = k > mine if reverse else k < mine
            so_far = combine(
                so_far, jax.tree.map(lambda part, own: part[k].astype(own.dtype), pieces, value)
            )
            inside = jax.tree.map(lambda new, old: jnp.where(passed, new, old), so_far, inside)
        before = combine(inside, before)
    return before


def in_blocks(value, dim, length):
    lengths = value.shape
    pieces = value.reshape(*lengths[:dim], length, lengths[dim] // length, *lengths[dim + 1 :])
    return jnp.moveaxis(pieces, dim, 0)


def sent_and_summed(value, axis, dim):
    length = lax.axis_size(axis)
    pieces = lax.all_to_all(in_blocks(value, dim, length), axis, 0, 0, tiled=True)
    return jnp.sum(pieces.astype(jnp.float32), axis=0)


def copy_for_each(value, axis):
    length = lax.axis_size(axis)
    return lax.all_to_all(
        jnp.broadcast_to(value[None], (length, *value.shape)), axis, 0, 0, tiled=True
    )


def taken_together(value, axis):
    return copy_for_each(value, axis).sum(axis=0)


def block_parts(c_block, b_block, dt_block, decay_block, reset_block):
    block_len = c_block.shape[0]
    running = jnp.cumsum(decay_block, axis=0)
    reset_count = jnp.cumsum(reset_block, axis=0)
    scores = lax.dot_general(
        c_block, b_block, (((1,), (1,)), ((), ())), preferred_element_type=jnp.float32
    )
    indices = jnp.arange(block_len, dtype=jnp.int32)
    allowed = (indices[:, None] >= indices[None, :]) & (
        reset_count[:, None] == reset_count[None, :]
    )
    log_gap = running.T[:, :, None] - running.T[:, None, :]
    mixing = (
        jnp.where(allowed[None], jnp.exp(jnp.minimum(log_gap, 0.0)), 0.0)
        * scores[None]
        * dt_block.T[:, None, :]
    )
    mixing = mixing.astype(jnp.bfloat16)
    end_count = reset_count[-1]
    carry_weight = jnp.where((reset_count == 0)[:, None], jnp.exp(running), 0.0)
    tail_weight = jnp.where(
        (reset_count == end_count)[:, None], jnp.exp(running[-1][None, :] - running), 0.0
    )
    block_decay = jnp.where(end_count == 0, jnp.exp(running[-1]), 0.0)
    return (mixing, carry_weight, tail_weight, block_decay)


def chain_link(earlier, later):
    return (earlier[0] * later[0], later[0][:, None, None] * earlier[1] + later[1])


def local(
    ssm_input,
    gate_z,
    b_proj,
    c_proj,
    step_size,
    log_decay,
    skip_d,
    norm_gain,
    w_out,
    d_out,
    game_lengths,
):
    seq_len = ssm_input.shape[1]
    local_width = ssm_input.shape[2]
    heads_here = step_size.shape[2]
    head_dim = local_width // heads_here
    state_dim = b_proj.shape[2]
    block_len = min(512, seq_len)
    count_blocks = seq_len // block_len
    total_width = local_width * lax.axis_size("chan")
    x_heads = ssm_input[0].reshape(seq_len, heads_here, head_dim)
    c_rows = c_proj[0]
    b_rows = b_proj[0]
    dt_rows = step_size[0]
    lengths = game_lengths[0]
    starts = jnp.cumsum(lengths) - lengths
    sequence_positions = lax.axis_index(SEQ) * seq_len + jnp.arange(seq_len, dtype=jnp.int32)
    resets = jnp.any(sequence_positions[:, None] == starts[None, :], axis=1).astype(jnp.int32)

    def blocked(array):
        return array.reshape((count_blocks, block_len) + array.shape[1:])

    zero_state = jnp.zeros((heads_here, state_dim, head_dim), jnp.float32)
    unit_decay = jnp.ones((heads_here,), jnp.float32)

    def forward_step(state_pair, block_inputs):
        local_state, before = state_pair
        x_block, c_block, b_block, dt_block, decay_block, reset_block = block_inputs
        mixing, carry_weight, tail_weight, block_decay = block_parts(
            c_block, b_block, dt_block, decay_block, reset_block
        )
        inside = jnp.einsum("hts,shp->thp", mixing, x_block, preferred_element_type=jnp.float32)
        carried = carry_weight[:, :, None] * jnp.einsum(
            "tn,hnp->thp", c_block.astype(jnp.float32), local_state
        )
        scaled = ((tail_weight * dt_block)[:, :, None] * x_block).astype(jnp.bfloat16)
        fresh_state = jnp.einsum("sn,shp->hnp", b_block, scaled, preferred_element_type=jnp.float32)
        new_pair = (block_decay[:, None, None] * local_state + fresh_state, before * block_decay)
        return (
            new_pair,
            (
                inside + carried,
                carry_weight * before[None, :],
                mixing,
                carry_weight,
                tail_weight,
                block_decay,
            ),
        )

    forward_inputs = (
        blocked(x_heads),
        blocked(c_rows),
        blocked(b_rows),
        blocked(dt_rows),
        blocked(log_decay[0]),
        blocked(resets),
    )
    (dev_state, dev_decay), (
        ssd_blocks,
        incoming_weight,
        mixings,
        carry_weights,
        tail_weights,
        block_decays,
    ) = lax.scan(forward_step, (zero_state, unit_decay), forward_inputs)
    _, incoming = prefix_by_axis(
        (dev_decay, dev_state), SEQ, chain_link, (unit_decay, zero_state), False
    )
    from_left = jnp.einsum("tn,hnp->thp", c_rows.astype(jnp.float32), incoming)
    ssd_out = (
        ssd_blocks.reshape(seq_len, heads_here, head_dim)
        + incoming_weight.reshape(seq_len, heads_here)[:, :, None] * from_left
    )
    ssd_out = ssd_out + skip_d[None, :, None] * x_heads.astype(jnp.float32)
    gate_act = jax.nn.silu(gate_z[0].astype(jnp.float32))
    gated = ssd_out.reshape(seq_len, local_width) * gate_act
    square_total = lax.psum(jnp.sum(gated * gated, axis=1), "chan")
    inv_rms = lax.rsqrt(square_total / total_width + NORM_EPS)
    normed = (gated * norm_gain).astype(jnp.bfloat16)
    w_cols = w_out
    projected = sent_and_summed(
        lax.dot_general(
            w_cols, normed, (((0,), (1,)), ((), ())), preferred_element_type=jnp.float32
        ).astype(jnp.bfloat16),
        "chan",
        0,
    ).T
    out = (inv_rms[:, None] * projected).astype(jnp.bfloat16)[None]
    cotangent = d_out[0]
    w_cols = w_out
    pulled = lax.dot_general(
        lax.all_gather(cotangent, "chan", axis=1, tiled=True),
        w_cols,
        (((1,), (1,)), ((), ())),
        preferred_element_type=jnp.float32,
    )
    out_dot = lax.psum(jnp.sum(cotangent.astype(jnp.float32) * projected, axis=1), "chan")
    d_normed = inv_rms[:, None] * pulled
    gain_local = jnp.sum(gated * d_normed, axis=0)
    d_ssd = (
        (norm_gain * d_normed - (inv_rms**3 * out_dot / total_width)[:, None] * gated) * gate_act
    ).astype(jnp.bfloat16)
    d_heads = d_ssd.reshape(seq_len, heads_here, head_dim)
    skip_local = jnp.sum(d_heads.astype(jnp.float32) * x_heads.astype(jnp.float32), axis=(0, 2))
    grad_gain, grad_skip = (taken_together(gain_local, SEQ_DP), taken_together(skip_local, SEQ_DP))

    def backward_step(state_pair, block_inputs):
        local_adjoint, later_decay = state_pair
        d_block, c_block, b_block, dt_block, mixing, carry_weight, tail_weight, block_decay = (
            block_inputs
        )
        inside = jnp.einsum("hts,thp->shp", mixing, d_block, preferred_element_type=jnp.float32)
        carried = (dt_block * tail_weight)[:, :, None] * jnp.einsum(
            "sn,hnp->shp", b_block.astype(jnp.float32), local_adjoint
        )
        weighted = (carry_weight[:, :, None] * d_block).astype(jnp.bfloat16)
        fresh_adjoint = jnp.einsum(
            "tn,thp->hnp", c_block, weighted, preferred_element_type=jnp.float32
        )
        new_pair = (
            fresh_adjoint + block_decay[:, None, None] * local_adjoint,
            later_decay * block_decay,
        )
        return (new_pair, (inside + carried, dt_block * tail_weight * later_decay[None, :]))

    backward_inputs = (
        blocked(d_heads),
        blocked(c_rows),
        blocked(b_rows),
        blocked(dt_rows),
        mixings,
        carry_weights,
        tail_weights,
        block_decays,
    )
    (dev_adjoint, _), (grad_blocks, outgoing_weight) = lax.scan(
        backward_step, (zero_state, unit_decay), backward_inputs, reverse=True
    )
    _, from_right = prefix_by_axis(
        (dev_decay, dev_adjoint), SEQ, chain_link, (unit_decay, zero_state), True
    )
    right_terms = jnp.einsum("sn,hnp->shp", b_rows.astype(jnp.float32), from_right)
    grad_heads = (
        grad_blocks.reshape(seq_len, heads_here, head_dim)
        + outgoing_weight.reshape(seq_len, heads_here)[:, :, None] * right_terms
    )
    grad_heads = grad_heads + skip_d[None, :, None] * d_heads.astype(jnp.float32)
    grad_x = grad_heads.astype(jnp.bfloat16).reshape(1, seq_len, local_width)
    return (out, grad_x, grad_gain, grad_skip)


def solution(mesh):
    finer = Mesh(
        mesh.devices.reshape(4, 8, mesh.shape["chan"], mesh.shape["dp"]),
        ("seq_0", "seq_1", "chan", "dp"),
    )
    return jax.shard_map(
        local,
        mesh=finer,
        in_specs=(
            P("dp", SEQ, "chan"),
            P("dp", SEQ, "chan"),
            P("dp", SEQ, None),
            P("dp", SEQ, None),
            P("dp", SEQ, "chan"),
            P("dp", SEQ, "chan"),
            P("chan"),
            P("chan"),
            P("chan", None),
            P("dp", SEQ, "chan"),
            P("dp", None),
        ),
        out_specs=(P("dp", SEQ, "chan"), P("dp", SEQ, "chan"), P("chan"), P("chan")),
        check_vma=False,
    )
```

profile of v0, /device:TPU:1, one launch (start us, length us, event | category | flops | bytes accessed | tf_op | source)
XLA Modules:
  0.0 204.7 jit_solution(17596666255649511182)
XLA Ops:
  7.3 1.0 reduce-window_clone.1
  8.3 0.7 subtract_bitcast_fusion
  9.1 0.2 broadcast_in_dim.163
  9.3 0.5 slice.212
  10.6 0.8 copy.86
  11.4 0.2 reduce_window_sum.27
  11.6 0.7 broadcast_compare_fusion.1
  12.2 0.8 copy.89
  13.2 0.1 copy.94
  13.4 0.9 fusion.16
  14.4 0.8 fusion.14
  15.3 13.8 %all-gather.3 = bf16[8,1,8]{2,1,0:T(2,128)(2,1)S(1)} all-gather(bf16[1,1,8]{2,1,0:T(2,128)(2,1)S(1)} %get-tuple-element.116), channel_id=1, replica_groups=mesh['seq_0'=4,'seq_1'=8,'chan'=8,'dp'=2] {'seq_1'}, dimensions={0}, use_global_device_ids=true | all-gather | bytes 144 | tf_op jit(solution)/shard_map/all_gather | solution.py:26
  29.1 0.5 convert_bitcast_fusion.2
  29.6 7.7 %all-gather.4 = bf16[4,1,8]{2,1,0:T(2,128)(2,1)S(1)} all-gather(bf16[1,1,8]{2,1,0:T(2,128)(2,1)S(1)} %get-tuple-element.121), channel_id=1, replica_groups=mesh['seq_0'=4,'seq_1'=8,'chan'=8,'dp'=2] {'seq_0'}, dimensions={0}, use_global_device_ids=true | all-gather | bytes 80 | tf_op jit(solution)/shard_map/all_gather | solution.py:26
  37.8 0.5 broadcast_select_fusion.7
  38.3 0.5 fusion.179
  38.9 0.1 fusion.154
  39.1 0.2 fusion.9
  39.3 18.3 %all-gather.9.cloned.1.call-done = bf16[64,128,64]{1,2,0:T(8,128)(2,1)} async-done(((bf16[8,128,64]{1,2,0:T(8,128)(2,1)}), bf16[64,128,64]{1,2,0:T(8,128)(2,1)}) %all-gather.9.cloned.1.call-update) | async-done | bytes 1048592 | tf_op jit(solution)/shard_map/all_gather | solution.py:26
  57.6 1.6 fusion.79
  59.3 9.9 %all_gather.41 = bf16[4,8,128,64]{2,3,1,0:T(8,128)(2,1)S(1)} all-gather(bf16[1,8,128,64]{2,3,1,0:T(8,128)(2,1)S(1)} %fusion.79), channel_id=1, replica_groups=mesh['seq_0'=4,'seq_1'=8,'chan'=8,'dp'=2] {'seq_0'}, dimensions={0}, use_global_device_ids=true | all-gather | bytes 655360 | tf_op jit(solution)/shard_map/all_gather | solution.py:26
  69.2 1.9 fusion.8
  71.2 0.9 multiply_reduce_fusion.1
  72.1 0.8 copy.97
  73.0 1.4 convolution_convert_fusion
  74.4 0.8 copy.110
  75.2 6.7 %all-to-all-start = ((bf16[8,256,128]{1,2,0:T(8,128)(2,1)}), bf16[8,256,128]{1,2,0:T(8,128)(2,1)S(1)}, u32[]{:S(2)}, u32[]{:S(2)}) async-start(bf16[8,256,128]{1,2,0:T(8,128)(2,1)} %bitcast.430), calls=%async_computation | async-start | bytes 1048576 | tf_op jit(solution)/shard_map/all_to_all | solution.py:49
  82.1 27.0 %all-gather.1 = bf16[1,128,2048]{2,1,0:T(8,128)(2,1)S(1)} all-gather(bf16[1,128,256]{2,1,0:T(8,128)(2,1)S(1)} %copy-done.6), channel_id=3, replica_groups=mesh['seq_0'=4,'seq_1'=8,'chan'=8,'dp'=2] {'chan'}, dimensions={2}, use_global_device_ids=true | all-gather | bytes 589824 | tf_op jit(solution)/shard_map/all_gather | solution.py:198
  109.1 0.9 fusion.88
  110.1 14.6 %all-reduce = (f32[128]{0:T(128)S(1)}, f32[128]{0:T(128)S(1)}) all-reduce(f32[128]{0:T(128)} %get-tuple-element.140, f32[128]{0:T(128)S(1)} %fusion.88), channel_id=1, replica_groups=mesh['seq_0'=4,'seq_1'=8,'chan'=8,'dp'=2] {'chan'}, use_global_device_ids=true, to_apply=%region_5.6 | all-reduce | flops 256 | bytes 2048 | tf_op jit(solution)/shard_map/psum | solution.py:183
  124.7 2.0 fusion.18
  127.0 0.8 fusion.13
  127.8 6.4 %all-gather.5 = bf16[4,1,8]{2,1,0:T(2,128)(2,1)S(1)} all-gather(bf16[1,1,8]{2,1,0:T(2,128)(2,1)S(1)} %copy-done.28), channel_id=1, replica_groups=mesh['seq_0'=4,'seq_1'=8,'chan'=8,'dp'=2] {'seq_0'}, dimensions={0}, use_global_device_ids=true | all-gather | bytes 80 | tf_op jit(solution)/shard_map/all_gather | solution.py:26
  134.2 0.2 fusion.7
  134.6 0.6 broadcast_in_dim.174
  135.2 21.9 %all-to-all-start.2 = ((f32[64,1,8]{2,1,0:T(1,128)}), f32[64,1,8]{2,1,0:T(1,128)S(1)}, u32[]{:S(2)}, u32[]{:S(2)}) async-start(f32[64,1,8]{2,1,0:T(1,128)} %broadcast_in_dim.174), calls=%async_computation.2 | async-start | bytes 65536 | tf_op jit(solution)/shard_map/all_to_all | solution.py:55
  157.1 9.2 %all-to-all-done.2 = f32[64,1,8]{2,1,0:T(1,128)S(1)} async-done(((f32[64,1,8]{2,1,0:T(1,128)}), f32[64,1,8]{2,1,0:T(1,128)S(1)}, u32[]{:S(2)}, u32[]{:S(2)}) %all-to-all-start.2) | async-done | bytes 2080 | tf_op jit(solution)/shard_map/all_to_all | solution.py:55
  166.4 0.7 broadcast_in_dim.173
  167.1 4.7 %all-to-all-start.1 = ((f32[64,1,512]{2,1,0:T(1,128)}), f32[64,1,512]{2,1,0:T(1,128)S(1)}, u32[]{:S(2)}, u32[]{:S(2)}) async-start(f32[64,1,512]{2,1,0:T(1,128)} %broadcast_in_dim.173), calls=%async_computation.1 | async-start | bytes 262144 | tf_op jit(solution)/shard_map/all_to_all | solution.py:55
  171.9 0.7 fusion.145
  172.6 0.6 reduce_sum.78
  173.2 9.0 %all-to-all-done.1 = f32[64,1,512]{2,1,0:T(1,128)S(1)} async-done(((f32[64,1,512]{2,1,0:T(1,128)}), f32[64,1,512]{2,1,0:T(1,128)S(1)}, u32[]{:S(2)}, u32[]{:S(2)}) %all-to-all-start.1) | async-done | bytes 131104 | tf_op jit(solution)/shard_map/all_to_all | solution.py:55
  182.2 0.7 reduce_sum.74
  183.0 1.6 fusion.62
  184.6 10.1 %all_gather.46 = bf16[4,8,128,64]{2,3,1,0:T(8,128)(2,1)S(1)} all-gather(bf16[1,8,128,64]{2,3,1,0:T(8,128)(2,1)S(1)} %fusion.62), channel_id=1, replica_groups=mesh['seq_0'=4,'seq_1'=8,'chan'=8,'dp'=2] {'seq_0'}, dimensions={0}, use_global_device_ids=true | all-gather | bytes 655360 | tf_op jit(solution)/shard_map/all_gather | solution.py:26
  194.7 1.9 fusion.6
  196.7 0.4 fusion.12
  197.1 0.8 copy.104
  (102 shorter events, 2.1 us)
Async XLA Ops:
  7.2 65.8 %copy-start = (bf16[512,2048]{1,0:T(8,128)(2,1)S(1)}, bf16[512,2048]{1,0:T(8,128)(2,1)}, u32[]{:S(2)}) copy-start(bf16[512,2048]{1,0:T(8,128)(2,1)} %param.19) | copy-start | bytes 6291460
  7.2 30.2 %copy-start.1 = (bf16[1,128,512]{2,1,0:T(8,128)(2,1)S(1)}, bf16[1,128,512]{2,1,0:T(8,128)(2,1)}, u32[]{:S(2)}) copy-start(bf16[1,128,512]{2,1,0:T(8,128)(2,1)} %param.11) | copy-start | bytes 393220
  7.2 7.2 %copy-start.4 = (bf16[1,128,128]{2,1,0:T(8,128)(2,1)S(1)}, bf16[1,128,128]{2,1,0:T(8,128)(2,1)}, u32[]{:S(2)}) copy-start(bf16[1,128,128]{2,1,0:T(8,128)(2,1)} %param.13) | copy-start | bytes 98308
  7.2 30.4 %copy-start.7 = (bf16[1,128,512]{2,1,0:T(8,128)(2,1)S(1)}, bf16[1,128,512]{2,1,0:T(8,128)(2,1)}, u32[]{:S(2)}) copy-start(bf16[1,128,512]{2,1,0:T(8,128)(2,1)} %param.12) | copy-start | bytes 393220
  7.2 31.7 %copy-start.2 = (bf16[1,128,128]{2,1,0:T(8,128)(2,1)S(1)}, bf16[1,128,128]{2,1,0:T(8,128)(2,1)}, u32[]{:S(2)}) copy-start(bf16[1,128,128]{2,1,0:T(8,128)(2,1)} %param.14) | copy-start | bytes 98308
  7.2 50.4 %all-gather.9.cloned.1.call-start = ((), (), s32[]{:S(2)}) async-start(), calls=%async_computation.3 | async-start | bytes 1179648 | tf_op jit(solution)/shard_map/all_gather | solution.py:26
  11.6 25.8 %copy-start.24 = (f32[8]{0:T(128)}, f32[8]{0:T(128)S(1)}, u32[]{:S(2)}) copy-start(f32[8]{0:T(128)S(1)} %fusion.160) | copy-start | bytes 100
  37.6 33.6 %copy-start.22 = (f32[8,128]{1,0:T(8,128)}, f32[8,128]{1,0:T(8,128)S(1)}, u32[]{:S(2)}) copy-start(f32[8,128]{1,0:T(8,128)S(1)} %copy.87) | copy-start | bytes 12292
  38.8 32.3 %copy-start.12 = (f32[8]{0:T(128)}, f32[8]{0:T(128)S(1)}, u32[]{:S(2)}) copy-start(f32[8]{0:T(128)S(1)} %get-tuple-element.125) | copy-start | bytes 100
  38.8 32.3 %copy-start.14 = (f32[8]{0:T(128)}, f32[8]{0:T(128)S(1)}, u32[]{:S(2)}) copy-start(f32[8]{0:T(128)S(1)} %get-tuple-element.126) | copy-start | bytes 100
  38.8 32.3 %copy-start.16 = (f32[8]{0:T(128)}, f32[8]{0:T(128)S(1)}, u32[]{:S(2)}) copy-start(f32[8]{0:T(128)S(1)} %get-tuple-element.127) | copy-start | bytes 100
  38.8 32.3 %copy-start.18 = (f32[8]{0:T(128)}, f32[8]{0:T(128)S(1)}, u32[]{:S(2)}) copy-start(f32[8]{0:T(128)S(1)} %get-tuple-element.128) | copy-start | bytes 100
  38.9 32.2 %copy-start.10 = (pred[128,128]{1,0:T(8,128)(4,1)}, pred[128,128]{1,0:T(8,128)(4,1)S(1)}, u32[]{:S(2)}) copy-start(pred[128,128]{1,0:T(8,128)(4,1)S(1)} %fusion.147) | copy-start | bytes 49156
  39.1 32.1 %copy-start.8 = (f32[128,128]{1,0:T(8,128)}, f32[128,128]{1,0:T(8,128)S(1)}, u32[]{:S(2)}) copy-start(f32[128,128]{1,0:T(8,128)S(1)} %fusion.154) | copy-start | bytes 196612
  69.2 2.0 copy-start.20
  69.2 2.0 copy-start.31
  71.1 1.8 copy-start.30
  74.4 7.7 %copy-start.6 = (bf16[1,128,256]{2,1,0:T(8,128)(2,1)S(1)}, bf16[1,128,256]{2,1,0:T(8,128)(2,1)}, u32[]{:S(2)}) copy-start(bf16[1,128,256]{2,1,0:T(8,128)(2,1)} %param.20) | copy-start | bytes 196612
  75.2 33.8 %all-to-all-start = ((bf16[8,256,128]{1,2,0:T(8,128)(2,1)}), bf16[8,256,128]{1,2,0:T(8,128)(2,1)S(1)}, u32[]{:S(2)}, u32[]{:S(2)}) async-start(bf16[8,256,128]{1,2,0:T(8,128)(2,1)} %bitcast.430), calls=%async_computation | async-start | bytes 1048576 | tf_op jit(solution)/shard_map/all_to_all | solution.py:49
  81.9 101.0 %all-gather.11.cloned.1.call-start = ((), (), s32[]{:S(2)}) async-start(), calls=%async_computation.4 | async-start | bytes 1179648 | tf_op jit(solution)/shard_map/all_gather | solution.py:26
  124.7 2.3 %copy-start.3 = (bf16[1,128,128]{2,1,0:T(8,128)(2,1)S(1)}, bf16[1,128,128]{2,1,0:T(8,128)(2,1)}, u32[]{:S(2)}) copy-start(bf16[1,128,128]{2,1,0:T(8,128)(2,1)} %param.14) | copy-start | bytes 98308
  124.7 2.3 %copy-start.25 = (f32[8]{0:T(128)S(1)}, f32[8]{0:T(128)}, u32[]{:S(2)}) copy-start(f32[8]{0:T(128)} %copy-done.24) | copy-start | bytes 100
  124.7 3.1 %copy-start.28 = (bf16[1,1,8]{2,1,0:T(2,128)(2,1)S(1)}, bf16[1,1,8]{2,1,0:T(2,128)(2,1)}, u32[]{:S(2)}) copy-start(bf16[1,1,8]{2,1,0:T(2,128)(2,1)} %get-tuple-element.120) | copy-start | bytes 52
  124.7 9.5 %copy-start.5 = (bf16[1,128,128]{2,1,0:T(8,128)(2,1)S(1)}, bf16[1,128,128]{2,1,0:T(8,128)(2,1)}, u32[]{:S(2)}) copy-start(bf16[1,128,128]{2,1,0:T(8,128)(2,1)} %param.13) | copy-start | bytes 98308
  126.7 56.2 %copy-start.13 = (f32[8]{0:T(128)S(1)}, f32[8]{0:T(128)}, u32[]{:S(2)}) copy-start(f32[8]{0:T(128)} %copy-done.12) | copy-start | bytes 100
  126.7 56.2 %copy-start.15 = (f32[8]{0:T(128)S(1)}, f32[8]{0:T(128)}, u32[]{:S(2)}) copy-start(f32[8]{0:T(128)} %copy-done.14) | copy-start | bytes 100
  126.7 56.2 %copy-start.17 = (f32[8]{0:T(128)S(1)}, f32[8]{0:T(128)}, u32[]{:S(2)}) copy-start(f32[8]{0:T(128)} %copy-done.16) | copy-start | bytes 100
  126.7 56.2 %copy-start.19 = (f32[8]{0:T(128)S(1)}, f32[8]{0:T(128)}, u32[]{:S(2)}) copy-start(f32[8]{0:T(128)} %copy-done.18) | copy-start | bytes 100
  126.7 56.2 %copy-start.26 = (f32[8]{0:T(128)S(1)}, f32[8]{0:T(128)}, u32[]{:S(2)}) copy-start(f32[8]{0:T(128)} %get-tuple-element.119) | copy-start | bytes 100
  126.8 56.2 %copy-start.27 = (f32[8]{0:T(128)S(1)}, f32[8]{0:T(128)}, u32[]{:S(2)}) copy-start(f32[8]{0:T(128)} %get-tuple-element.122) | copy-start | bytes 100
  126.8 67.9 %copy-start.29 = (f32[8]{0:T(128)S(1)}, f32[8]{0:T(128)}, u32[]{:S(2)}) copy-start(f32[8]{0:T(128)} %get-tuple-element.117) | copy-start | bytes 100
  135.2 31.1 %all-to-all-start.2 = ((f32[64,1,8]{2,1,0:T(1,128)}), f32[64,1,8]{2,1,0:T(1,128)S(1)}, u32[]{:S(2)}, u32[]{:S(2)}) async-start(f32[64,1,8]{2,1,0:T(1,128)} %broadcast_in_dim.174), calls=%async_computation.2 | async-start | bytes 65536 | tf_op jit(solution)/shard_map/all_to_all | solution.py:55
  167.1 15.2 %all-to-all-start.1 = ((f32[64,1,512]{2,1,0:T(1,128)}), f32[64,1,512]{2,1,0:T(1,128)S(1)}, u32[]{:S(2)}, u32[]{:S(2)}) async-start(f32[64,1,512]{2,1,0:T(1,128)} %broadcast_in_dim.173), calls=%async_computation.1 | async-start | bytes 262144 | tf_op jit(solution)/shard_map/all_to_all | solution.py:55
  194.7 2.0 copy-start.9
  194.7 2.0 copy-start.11
  194.7 2.0 copy-start.21
  194.7 2.0 copy-start.23
  194.7 2.0 copy-start.32
Sparse Core Ops, SparseCore 0:
  15.4 42.1 all-gather.8
  127.9 46.2 all-gather.10
where the time goes:
time: 207 us; the launch traced here: 205 us
  blocking collectives  89.4 us (43%)
  waiting for transfers between devices  36.6 us (18%)
  starting transfers between devices  33.3 us (16%)
  between operations  15.3 us (7%)
  other arithmetic  12 us (6%)
  matrix products  10.7 us (5%)
  local copies, waits for them, and re-layouts  7.31 us (4%)
    all_gather x5, blocking collectives, prefix_by_axis(): lax.all_gather(part.astype(kind), axis)  47.9 us
    all_gather x1, blocking collectives, local(): lax.all_gather(cotangent, 'chan', axis=1, tiled=True)  27 us
    all_to_all x2, starting transfers between devices, copy_for_each(): lax.all_to_all(jnp.broadcast_to(value[None], (length, *value.shape)), axi...  26.6 us
    all_gather x2, waiting for transfers between devices, prefix_by_axis(): lax.all_gather(part.astype(kind), axis)  18.3 us
    all_to_all x2, waiting for transfers between devices, copy_for_each(): lax.all_to_all(jnp.broadcast_to(value[None], (length, *value.shape)), axi...  18.2 us
    psum x1, blocking collectives, local(): square_total = lax.psum(jnp.sum(gated * gated, axis=1), 'chan')  14.6 us
    all_to_all x1, starting transfers between devices, sent_and_summed(): lax.all_to_all(in_blocks(value, dim, length), axis, 0, 0, tiled=True)  6.67 us
  transfers between devices with their start and end apart: 5, of which 3 were waited for; matrix products, arithmetic and copies ran while one was open for 3% of the time, Pallas kernels for 0%

commit v1 on v0

v1 whole, which is shorter than its diff:
```python
import jax
import jax.numpy as jnp
from jax import lax
from jax.experimental import pallas as pl
from jax.experimental.pallas import tpu as pltpu
from jax.sharding import Mesh
from jax.sharding import PartitionSpec as P

SEQ = ("seq_0", "seq_1")
NORM_EPS = 1e-05
MESH = pl.DeviceIdType.MESH
HIGH = lax.Precision.HIGHEST
F32 = jnp.float32
BF16 = jnp.bfloat16


def dot(a, b, ca=1, cb=0, precision=None):
    return lax.dot_general(
        a, b, (((ca,), (cb,)), ((), ())), precision=precision, preferred_element_type=F32
    )


class Exchange:
    def __init__(self, axis, size, source, landing, sends, receives):
        self.axis, self.size, self.me = axis, size, lax.axis_index(axis)
        self.source, self.landing = source, landing
        self.sends, self.receives = sends, receives

    def copy(self, k, slot):
        peer = lax.rem(self.me + k, self.size)
        return pltpu.make_async_remote_copy(
            src_ref=self.source(peer),
            dst_ref=self.landing.at[slot(peer)],
            send_sem=self.sends.at[k - 1],
            recv_sem=self.receives.at[slot(peer)],
            device_id={self.axis: peer},
            device_id_type=MESH,
        )

    def start(self):
        for k in range(1, self.size):
            self.copy(k, lambda peer: self.me).start()

    def receive(self, k):
        self.copy(k, lambda peer: peer).wait_recv()

    def receive_all(self):
        for k in range(1, self.size):
            self.receive(k)

    def finish(self):
        for k in range(1, self.size):
            self.copy(k, lambda peer: self.me).wait_send()


class Shift:
    def __init__(self, axis, size, distance, source, landing, send, receive):
        peer = lax.rem(lax.axis_index(axis) + distance + size, size)
        self.copy = pltpu.make_async_remote_copy(
            src_ref=source,
            dst_ref=landing,
            send_sem=send,
            recv_sem=receive,
            device_id={axis: peer},
            device_id_type=MESH,
        )
        self.start, self.receive, self.finish = (
            self.copy.start,
            self.copy.wait_recv,
            self.copy.wait_send,
        )


def kernel(
    nx,
    ny,
    nz,
    nd,
    length_ref,
    skip_ref,
    x_hbm,
    z_hbm,
    b_hbm,
    c_hbm,
    dt_hbm,
    ld_hbm,
    gain_hbm,
    w_hbm,
    dout_hbm,
    out_ref,
    gx_ref,
    gg_ref,
    gs_ref,
    x_ref,
    z_ref,
    b_ref,
    c_ref,
    dt_ref,
    ld_ref,
    gain_ref,
    w_ref,
    dout_all,
    mix_back,
    decay_all,
    state_out,
    state_in,
    row_state,
    row_in,
    row_decay,
    decay_in,
    back_out,
    back_in,
    adj_out,
    adj_in,
    adj_row,
    adj_row_in,
    adj_back_out,
    adj_back_in,
    stat_all,
    proj_out,
    proj_in,
    sums_y,
    sums_x,
    sums_d,
    load_sem,
    sem_y,
    sem_z,
    sem_x,
    sem_d,
    sem_shift,
):
    length, width = x_ref.shape
    heads = dt_ref.shape[1]
    head_dim = width // heads
    pairs = heads // 2
    lanes = 2 * head_dim
    rows = state_in.shape[1]
    total = width * nz
    me_x, me_y, me_z, me_d = (lax.axis_index(a) for a in ("seq_0", "seq_1", "chan", "dp"))

    loads = {}
    for slot, (name, source, target) in enumerate(
        (
            ("ld", ld_hbm, ld_ref),
            ("dt", dt_hbm, dt_ref),
            ("x", x_hbm, x_ref),
            ("b", b_hbm, b_ref),
            ("dout", dout_hbm, dout_all.at[me_z]),
            ("c", c_hbm, c_ref),
            ("z", z_hbm, z_ref),
            ("gain", gain_hbm, gain_ref),
            ("w", w_hbm, w_ref),
        )
    ):
        loads[name] = pltpu.make_async_copy(source, target, load_sem.at[slot])
        loads[name].start()

    barrier = pltpu.get_barrier_semaphore()
    for axis, size, me in (
        ("seq_1", ny, me_y),
        ("chan", nz, me_z),
        ("seq_0", nx, me_x),
        ("dp", nd, me_d),
    ):
        for k in range(1, size):
            pl.semaphore_signal(
                barrier, inc=1, device_id={axis: lax.rem(me + k, size)}, device_id_type=MESH
            )

    def over_y(index, source, landing):
        return Exchange("seq_1", ny, source, landing, sem_y.at[0, index], sem_y.at[1, index])

    def over_z(index, source, landing):
        return Exchange("chan", nz, source, landing, sem_z.at[0, index], sem_z.at[1, index])

    def shift_x(index, distance, source, landing):
        return Shift(
            "seq_0", nx, distance, source, landing, sem_shift.at[0, index], sem_shift.at[1, index]
        )

    decay_send = over_y(0, lambda peer: decay_all.at[me_y], decay_all)
    state_send = over_y(1, lambda peer: state_out.at[peer], state_in)
    back_send = over_y(2, lambda peer: back_out.at[peer], back_in)
    adj_send = over_y(3, lambda peer: adj_out.at[peer], adj_in)
    adj_back_send = over_y(4, lambda peer: adj_back_out.at[peer], adj_back_in)
    sums_y_send = over_y(5, lambda peer: sums_y.at[me_y], sums_y)
    dout_send = over_z(0, lambda peer: dout_all.at[me_z], dout_all)
    stat_send = over_z(1, lambda peer: stat_all.at[me_z], stat_all)
    proj_send = over_z(2, lambda peer: proj_out.at[peer], proj_in)
    sums_x_send = Exchange(
        "seq_0", nx, lambda peer: sums_x.at[me_x], sums_x, sem_x.at[0], sem_x.at[1]
    )
    sums_d_send = Exchange("dp", nd, lambda peer: sums_d.at[me_d], sums_d, sem_d.at[0], sem_d.at[1])
    row_sends = [shift_x(k, k + 1, row_state, row_in.at[k]) for k in range(2)]
    adj_row_sends = [shift_x(2 + k, -1 - k, adj_row, adj_row_in.at[k]) for k in range(2)]
    decay_sends = [shift_x(4, 1, row_decay, decay_in.at[0]), shift_x(5, -1, row_decay, decay_in.at[1])]

    base = (me_x * ny + me_y) * length
    first = length_ref[0, 0]
    second = first + length_ref[0, 1]
    third = second + length_ref[0, 2]

    def reset_count(position):
        count = jnp.zeros(position.shape, jnp.int32)
        for start in (jnp.int32(0), first, second, third):
            here = jnp.full(position.shape, start - base, jnp.int32)
            count = count + ((here >= 0) & (here <= position)).astype(jnp.int32)
        return count

    at_row = lax.broadcasted_iota(jnp.int32, (length, length), 0)
    at_col = lax.broadcasted_iota(jnp.int32, (length, length), 1)
    count_row = reset_count(at_row)
    count_col = reset_count(at_col)
    count_heads = reset_count(lax.broadcasted_iota(jnp.int32, (length, heads), 0))
    count_end = reset_count(jnp.full((length, heads), length - 1, jnp.int32))
    not_later = (at_row >= at_col).astype(F32)
    spread = (
        lax.broadcasted_iota(jnp.int32, (heads, width), 1) // head_dim
        == lax.broadcasted_iota(jnp.int32, (heads, width), 0)
    ).astype(F32)

    loads["ld"].wait()
    loads["dt"].wait()
    dt = dt_ref[...]
    running = dot(not_later, ld_ref[...], precision=HIGH)
    running_end = running[length - 1 :, :]
    carry_weight = jnp.where(count_heads == 0, jnp.exp(running), 0.0)
    tail_weight = jnp.where(count_heads == count_end, jnp.exp(running_end - running), 0.0)
    block_decay = jnp.where(count_end[:8] == 0, jnp.exp(jnp.broadcast_to(running_end, (8, heads))), 0.0)
    wide = dot(
        jnp.concatenate([tail_weight * dt, carry_weight, block_decay], axis=0), spread, precision=HIGH
    )
    tail_wide, carry_wide = wide[:length], wide[length : 2 * length]
    decay_all[me_y] = wide[2 * length : 2 * length + 1]
    loads["x"].wait()
    loads["b"].wait()
    x = x_ref[...].astype(F32)
    b = b_ref[...]
    fresh = dot(b, (tail_wide * x).astype(BF16), 0, 0).astype(BF16)
    fresh = fresh.reshape(ny, rows, width)
    state_out[...] = fresh
    state_in[me_y] = state_out[me_y]

    pl.semaphore_wait(barrier, (nx - 1) + (ny - 1) + (nz - 1) + (nd - 1))
    decay_send.start()
    state_send.start()
    loads["dout"].wait()
    dout_send.start()

    running_t = dot(ld_ref[...], not_later, 0, 1, precision=HIGH)
    dt_t = dot(dt, (at_row == at_col).astype(F32), 0, 0, precision=HIGH)
    loads["c"].wait()
    c = c_ref[...]
    same_game = count_row == count_col
    scores = jnp.where((at_row >= at_col) & same_game, dot(c, b, 1, 1), 0.0)
    scores_t = jnp.where((at_col >= at_row) & same_game, dot(b, c, 1, 1), 0.0)
    low_lane = lax.broadcasted_iota(jnp.int32, (length, lanes), 1) < head_dim

    def halves(tile):
        return jnp.concatenate([jnp.where(low_lane, tile, 0), jnp.where(low_lane, 0, tile)], axis=0)

    inside = []
    for pair in range(pairs):
        mixes, mixes_t = [], []
        for h in (2 * pair, 2 * pair + 1):
            column = jnp.broadcast_to(running[:, h : h + 1], (length, length))
            line = jnp.broadcast_to(running_t[h : h + 1], (length, length))
            mixes.append(
                (jnp.exp(jnp.minimum(column - line, 0.0)) * scores * dt_t[h : h + 1]).astype(BF16)
            )
            mixes_t.append(
                (jnp.exp(jnp.minimum(line - column, 0.0)) * scores_t * dt[:, h : h + 1]).astype(BF16)
            )
        mix_back[pair] = jnp.concatenate(mixes_t, axis=1)
        tile = x_ref[:, pair * lanes : (pair + 1) * lanes].astype(F32)
        inside.append(dot(jnp.concatenate(mixes, axis=1), halves(tile).astype(BF16)))
    inside = jnp.concatenate(inside, axis=1)
    head_of = lax.broadcasted_iota(jnp.int32, (1, width), 1) // head_dim
    skip = jnp.zeros((1, width), F32)
    for h in range(heads):
        skip = jnp.where(head_of == h, skip_ref[h], skip)
    inside = inside + skip * x
    loads["z"].wait()
    gate = z_ref[...].astype(F32)
    act = gate / (1.0 + jnp.exp(-gate))

    decay_send.receive_all()
    row_product = decay_all[0]
    for k in range(1, ny):
        row_product = row_product * decay_all[k]
    row_decay[...] = row_product
    for shift in decay_sends:
        shift.start()
    state_send.receive_all()
    state = state_in[0].astype(F32)
    for k in range(1, ny):
        state = decay_all[k] * state + state_in[k].astype(F32)
    row_state[...] = state.astype(BF16)
    for shift in row_sends:
        shift.start()
    loads["w"].wait()
    loads["gain"].wait()
    gain = gain_ref[...]
    for shift in decay_sends:
        shift.receive()
    for shift in row_sends:
        shift.receive()
    nearer = jnp.where(me_x >= 1, 1.0, 0.0)
    further = jnp.where(me_x >= 2, 1.0, 0.0)
    state = nearer * row_in[0].astype(F32) + further * (decay_in[0] * row_in[1].astype(F32))
    for k in range(ny):
        back_out[k] = state.astype(BF16)
        if k < ny - 1:
            state = decay_all[k] * state + state_in[k].astype(F32)
    back_in[me_y] = back_out[me_y]
    back_send.start()

    share = dout_all.shape[2]

    def columns(peer):
        return pl.ds(pl.multiple_of(peer * share, share), share)

    pulled = dot(dout_all[me_z], w_ref[:, columns(me_z)], 1, 1)
    for k in range(1, nz):
        dout_send.receive(k)
        peer = lax.rem(me_z + k, nz)
        pulled = pulled + dot(dout_all[peer], w_ref[:, columns(peer)], 1, 1)

    back_send.receive_all()
    from_left = dot(c, back_in[...].reshape(ny * rows, width))
    gated = (inside + carry_wide * from_left) * act
    normed = (gated * gain).astype(BF16)

    def over_features(values):
        part = values[:, :length]
        for k in range(1, width // length):
            part = part + values[:, k * length : (k + 1) * length]
        return jnp.sum(part.T, axis=0, keepdims=True)

    stat_all[me_z] = jnp.concatenate(
        [over_features(gated * gated), over_features(normed.astype(F32) * pulled)], axis=0
    )
    stat_send.start()
    for k in range(1, nz):
        peer = lax.rem(me_z + k, nz)
        proj_out[peer] = dot(normed, w_ref[:, columns(peer)]).astype(BF16)
        proj_send.copy(k, lambda peer: me_z).start()
    projected = dot(normed, w_ref[:, columns(me_z)])
    stat_send.receive_all()
    stats = stat_all[0]
    for k in range(1, nz):
        stats = stats + stat_all[k]
    inv_line = lax.rsqrt(stats[0:1] / total + NORM_EPS)
    pull_line = inv_line * inv_line * inv_line * stats[1:2] / total

    def down(line):
        return jnp.broadcast_to(line, (length, length)).T

    def across(tile):
        return jnp.concatenate([tile] * (width // length), axis=1)

    inv = down(inv_line)
    d_normed = across(inv) * pulled
    d_ssd = ((gain * d_normed - across(down(pull_line)) * gated) * act).astype(BF16)
    d_wide = d_ssd.astype(F32)
    adjoint = dot(c, (carry_wide * d_wide).astype(BF16), 0, 0).astype(BF16)
    adj_out[...] = adjoint.reshape(ny, rows, width)
    adj_in[me_y] = adj_out[me_y]
    adj_send.start()

    gain_part = jnp.sum(gated * d_normed, axis=0, keepdims=True)
    skip_part = jnp.sum(d_wide * x, axis=0, keepdims=True)
    fold = (
        lax.broadcasted_iota(jnp.int32, (width, length), 0) // head_dim
        == lax.broadcasted_iota(jnp.int32, (width, length), 1)
    ).astype(F32)
    skip_part = dot(jnp.broadcast_to(skip_part, (8, width)), fold, precision=HIGH)[:1]
    sums_y[me_y] = jnp.concatenate([gain_part, skip_part], axis=1)
    sums_y_send.start()

    inside_t = []
    for pair in range(pairs):
        tile = d_wide[:, pair * lanes : (pair + 1) * lanes]
        inside_t.append(dot(mix_back[pair], halves(tile).astype(BF16)))
    grad = jnp.concatenate(inside_t, axis=1) + skip * d_wide

    adj_send.receive_all()
    later = adj_in[ny - 1].astype(F32)
    for k in reversed(range(ny - 1)):
        later = decay_all[k] * later + adj_in[k].astype(F32)
    adj_row[...] = later.astype(BF16)
    for shift in adj_row_sends:
        shift.start()

    sums_y_send.receive_all()
    sums = sums_y[0]
    for k in range(1, ny):
        sums = sums + sums_y[k]
    sums_x[me_x] = sums
    sums_x_send.start()

    for shift in adj_row_sends:
        shift.receive()
    nearer = jnp.where(me_x < nx - 1, 1.0, 0.0)
    further = jnp.where(me_x < nx - 2, 1.0, 0.0)
    later = nearer * adj_row_in[0].astype(F32) + further * (decay_in[1] * adj_row_in[1].astype(F32))
    for k in reversed(range(ny)):
        adj_back_out[k] = later.astype(BF16)
        if k > 0:
            later = decay_all[k] * later + adj_in[k].astype(F32)
    adj_back_in[me_y] = adj_back_out[me_y]
    adj_back_send.start()

    sums_x_send.receive_all()
    sums = sums_x[0]
    for k in range(1, nx):
        sums = sums + sums_x[k]
    sums_d[me_d] = sums
    sums_d_send.start()

    for k in range(1, nz):
        proj_send.receive(k)
        projected = projected + proj_in[lax.rem(me_z + k, nz)].astype(F32)
    out_ref[...] = (jnp.concatenate([inv] * (share // length), axis=1) * projected).astype(BF16)

    sums_d_send.receive_all()
    sums = sums_d[0] + sums_d[1]
    gg_ref[...] = sums[:, :width]
    gs_ref[...] = sums[:, width:]

    adj_back_send.receive_all()
    right = dot(b, adj_back_in[...].reshape(ny * rows, width))
    gx_ref[...] = (grad + tail_wide * right).astype(BF16)

    for sent in (
        decay_send,
        state_send,
        back_send,
        adj_send,
        adj_back_send,
        sums_y_send,
        dout_send,
        stat_send,
        proj_send,
        sums_x_send,
        sums_d_send,
        *row_sends,
        *adj_row_sends,
        *decay_sends,
    ):
        sent.finish()


def mixer(
    sizes,
    ssm_input,
    gate_z,
    b_proj,
    c_proj,
    step_size,
    log_decay,
    skip_d,
    norm_gain,
    w_out,
    d_out,
    game_lengths,
):
    nx, ny, nz, nd = sizes
    length, width = ssm_input.shape[1:]
    heads = step_size.shape[2]
    state_dim = b_proj.shape[2]
    share = d_out.shape[2]
    rows = state_dim // ny
    pack = width + length

    def body(*refs):
        return kernel(nx, ny, nz, nd, *refs)

    hbm = pl.BlockSpec(memory_space=pltpu.HBM)
    smem = pl.BlockSpec(memory_space=pltpu.SMEM)
    vmem = pl.BlockSpec(memory_space=pltpu.VMEM)
    dma = pltpu.SemaphoreType.DMA
    out, grad_x, gain_sum, skip_sum = pl.pallas_call(
        body,
        out_shape=(
            jax.ShapeDtypeStruct((length, share), BF16),
            jax.ShapeDtypeStruct((length, width), BF16),
            jax.ShapeDtypeStruct((1, width), F32),
            jax.ShapeDtypeStruct((1, length), F32),
        ),
        in_specs=[smem, smem] + [hbm] * 9,
        out_specs=(vmem, vmem, vmem, vmem),
        scratch_shapes=[
            pltpu.VMEM((length, width), BF16),
            pltpu.VMEM((length, width), BF16),
            pltpu.VMEM((length, state_dim), BF16),
            pltpu.VMEM((length, state_dim), BF16),
            pltpu.VMEM((length, heads), F32),
            pltpu.VMEM((length, heads), F32),
            pltpu.VMEM((1, width), F32),
            pltpu.VMEM(w_out.shape, BF16),
            pltpu.VMEM((nz, length, share), BF16),
            pltpu.VMEM((heads // 2, length, 2 * length), BF16),
            pltpu.VMEM((ny, 1, width), F32),
            pltpu.VMEM((ny, rows, width), BF16),
            pltpu.VMEM((ny, rows, width), BF16),
            pltpu.VMEM((rows, width), BF16),
            pltpu.VMEM((2, rows, width), BF16),
            pltpu.VMEM((1, width), F32),
            pltpu.VMEM((2, 1, width), F32),
            pltpu.VMEM((ny, rows, width), BF16),
            pltpu.VMEM((ny, rows, width), BF16),
            pltpu.VMEM((ny, rows, width), BF16),
            pltpu.VMEM((ny, rows, width), BF16),
            pltpu.VMEM((rows, width), BF16),
            pltpu.VMEM((2, rows, width), BF16),
            pltpu.VMEM((ny, rows, width), BF16),
            pltpu.VMEM((ny, rows, width), BF16),
            pltpu.VMEM((nz, 2, length), F32),
            pltpu.VMEM((nz, length, share), BF16),
            pltpu.VMEM((nz, length, share), BF16),
            pltpu.VMEM((ny, 1, pack), F32),
            pltpu.VMEM((nx, 1, pack), F32),
            pltpu.VMEM((nd, 1, pack), F32),
            dma((9,)),
            dma((2, 6, ny)),
            dma((2, 3, nz)),
            dma((2, nx)),
            dma((2, nd)),
            dma((2, 6)),
        ],
        compiler_params=pltpu.CompilerParams(
            collective_id=0, has_side_effects=True, vmem_limit_bytes=48 * 1024 * 1024
        ),
        name="mixer",
    )(
        game_lengths,
        skip_d,
        ssm_input[0],
        gate_z[0],
        b_proj[0],
        c_proj[0],
        step_size[0],
        log_decay[0],
        norm_gain[None],
        w_out,
        d_out[0],
    )
    return (out[None], grad_x[None], gain_sum[0], skip_sum[0, :heads])


def solution(mesh):
    nz, nd = mesh.shape["chan"], mesh.shape["dp"]
    ny = 8
    nx = mesh.shape["seq"] // ny
    finer = Mesh(mesh.devices.reshape(nx, ny, nz, nd), ("seq_0", "seq_1", "chan", "dp"))

    def local(*args):
        return mixer((nx, ny, nz, nd), *args)

    return jax.shard_map(
        local,
        mesh=finer,
        in_specs=(
            P("dp", SEQ, "chan"),
            P("dp", SEQ, "chan"),
            P("dp", SEQ, None),
            P("dp", SEQ, None),
            P("dp", SEQ, "chan"),
            P("dp", SEQ, "chan"),
            P("chan"),
            P("chan"),
            P("chan", None),
            P("dp", SEQ, "chan"),
            P("dp", None),
        ),
        out_specs=(P("dp", SEQ, "chan"), P("dp", SEQ, "chan"), P("chan"), P("chan")),
        check_vma=False,
    )
```

time: 207 us -> 66.1 us (0.32)
  the two profiles are of different devices: /device:TPU:1 before, /device:TPU:6 now
where the time goes in v1:
time: 66.1 us; the launch traced here: 65.7 us
  Pallas kernels  53.3 us (81%)
  local copies, waits for them, and re-layouts  11.7 us (18%)
    pallas_call x1, Pallas kernels, mixer(): pl.pallas_call(body, out_shape=(jax.ShapeDtypeStruct((length, share), BF1...  53.3 us
    unnamed x23, local copies, waits for them, and re-layouts  11.2 us

profile of v1, /device:TPU:6, one launch (start us, length us, event | category | flops | bytes accessed | tf_op | source)
XLA Modules:
  0.0 65.7 jit_solution(6200571291895367908)
XLA Ops:
  0.6 0.8 %copy.15 = f32[1,128,8]{2,1,0:T(8,128)S(1)} copy(f32[1,128,8]{1,2,0:T(8,128)} %param.15) | data formatting | bytes 8192 | tf_op args[4]
  1.4 0.8 %copy.16 = f32[1,128,8]{2,1,0:T(8,128)S(1)} copy(f32[1,128,8]{1,2,0:T(8,128)} %param.16) | data formatting | bytes 8192 | tf_op args[5]
  2.2 0.0 copy-start
  2.2 1.6 %copy-done = bf16[512,2048]{1,0:T(8,128)(2,1)S(1)} copy-done((bf16[512,2048]{1,0:T(8,128)(2,1)S(1)}, bf16[512,2048]{1,0:T(8,128)(2,1)}, u32[]{:S(2)}) %copy-start) | copy-done | bytes 2097176
  3.8 0.0 copy-start.1
  3.8 0.9 %copy-done.1 = bf16[1,128,512]{2,1,0:T(8,128)(2,1)S(1)} copy-done((bf16[1,128,512]{2,1,0:T(8,128)(2,1)S(1)}, bf16[1,128,512]{2,1,0:T(8,128)(2,1)}, u32[]{:S(2)}) %copy-start.1) | copy-done | bytes 131096
  4.7 0.0 copy-start.2
  4.7 0.9 %copy-done.2 = bf16[1,128,512]{2,1,0:T(8,128)(2,1)S(1)} copy-done((bf16[1,128,512]{2,1,0:T(8,128)(2,1)S(1)}, bf16[1,128,512]{2,1,0:T(8,128)(2,1)}, u32[]{:S(2)}) %copy-start.2) | copy-done | bytes 131096
  5.6 0.0 copy-start.3
  5.6 0.8 %copy-done.3 = bf16[1,128,256]{2,1,0:T(8,128)(2,1)S(1)} copy-done((bf16[1,128,256]{2,1,0:T(8,128)(2,1)S(1)}, bf16[1,128,256]{2,1,0:T(8,128)(2,1)}, u32[]{:S(2)}) %copy-start.3) | copy-done | bytes 65560
  6.4 0.0 copy-start.4
  6.4 0.8 %copy-done.4 = bf16[1,128,128]{2,1,0:T(8,128)(2,1)S(1)} copy-done((bf16[1,128,128]{2,1,0:T(8,128)(2,1)S(1)}, bf16[1,128,128]{2,1,0:T(8,128)(2,1)}, u32[]{:S(2)}) %copy-start.4) | copy-done | bytes 32792
  7.2 0.0 copy-start.5
  7.2 0.8 %copy-done.5 = bf16[1,128,128]{2,1,0:T(8,128)(2,1)S(1)} copy-done((bf16[1,128,128]{2,1,0:T(8,128)(2,1)S(1)}, bf16[1,128,128]{2,1,0:T(8,128)(2,1)}, u32[]{:S(2)}) %copy-start.5) | copy-done | bytes 32792
  8.0 0.0 copy-start.6
  8.0 0.7 %copy-done.6 = f32[512]{0:T(512)S(1)} copy-done((f32[512]{0:T(512)S(1)}, f32[512]{0:T(512)}, u32[]{:S(2)}) %copy-start.6) | copy-done | bytes 2072
  8.6 0.0 copy-start.7
  8.6 0.7 copy-done.7
  9.3 0.0 copy-start.8
  9.3 0.7 copy-done.8
  10.0 53.3 %mixer.1 = (bf16[128,256]{1,0:T(8,128)(2,1)S(1)}, bf16[128,512]{1,0:T(8,128)(2,1)S(1)}, f32[1,512]{1,0:T(1,128)S(1)}, f32[1,128]{1,0:T(1,128)S(1)}) custom-call(s32[1,4]{1,0:T(1,128)S(1)} %copy-done.7, f32[8]{0:T(128)S(1)} %copy-done.8, bf16[128,512]{1,0:T(8,128)(2,1)S(1)} %bitcast.15, bf16[128,512]{1,0:T(8,128)(2,1)S(1)} %bitcast.16, ...), custom_call_target="tpu_custom_call" | custom-call | tf_op jit(solution)/shard_map/mixer/pallas_call | solution.py:483
  63.3 0.5 slice_bitcast_fusion
  63.8 0.6 copy.20
  64.4 0.7 copy.21
  65.1 0.6 copy.22
Async XLA Ops:
  2.2 1.6 %copy-start = (bf16[512,2048]{1,0:T(8,128)(2,1)S(1)}, bf16[512,2048]{1,0:T(8,128)(2,1)}, u32[]{:S(2)}) copy-start(bf16[512,2048]{1,0:T(8,128)(2,1)} %refs_9_.1) | copy-start | bytes 6291460
  3.8 0.9 %copy-start.1 = (bf16[1,128,512]{2,1,0:T(8,128)(2,1)S(1)}, bf16[1,128,512]{2,1,0:T(8,128)(2,1)}, u32[]{:S(2)}) copy-start(bf16[1,128,512]{2,1,0:T(8,128)(2,1)} %param.11) | copy-start | bytes 393220
  4.7 0.9 %copy-start.2 = (bf16[1,128,512]{2,1,0:T(8,128)(2,1)S(1)}, bf16[1,128,512]{2,1,0:T(8,128)(2,1)}, u32[]{:S(2)}) copy-start(bf16[1,128,512]{2,1,0:T(8,128)(2,1)} %param.12) | copy-start | bytes 393220
  5.6 0.8 %copy-start.3 = (bf16[1,128,256]{2,1,0:T(8,128)(2,1)S(1)}, bf16[1,128,256]{2,1,0:T(8,128)(2,1)}, u32[]{:S(2)}) copy-start(bf16[1,128,256]{2,1,0:T(8,128)(2,1)} %param.20) | copy-start | bytes 196612
  6.4 0.8 %copy-start.4 = (bf16[1,128,128]{2,1,0:T(8,128)(2,1)S(1)}, bf16[1,128,128]{2,1,0:T(8,128)(2,1)}, u32[]{:S(2)}) copy-start(bf16[1,128,128]{2,1,0:T(8,128)(2,1)} %param.13) | copy-start | bytes 98308
  7.2 0.8 %copy-start.5 = (bf16[1,128,128]{2,1,0:T(8,128)(2,1)S(1)}, bf16[1,128,128]{2,1,0:T(8,128)(2,1)}, u32[]{:S(2)}) copy-start(bf16[1,128,128]{2,1,0:T(8,128)(2,1)} %param.14) | copy-start | bytes 98308
  8.0 0.7 %copy-start.6 = (f32[512]{0:T(512)S(1)}, f32[512]{0:T(512)}, u32[]{:S(2)}) copy-start(f32[512]{0:T(512)} %param.18) | copy-start | bytes 6148
  8.6 0.7 copy-start.7
  9.3 0.7 copy-start.8

commit v2 on v1

--- a/solution.py
+++ b/solution.py
@@ -8,6 +8,7 @@
 
 SEQ = ("seq_0", "seq_1")
 NORM_EPS = 1e-05
+VMEM_LIMIT = 48 * 1024 * 1024
 MESH = pl.DeviceIdType.MESH
 HIGH = lax.Precision.HIGHEST
 F32 = jnp.float32
@@ -76,8 +77,8 @@
     ny,
     nz,
     nd,
-    length_ref,
-    skip_ref,
+    length_hbm,
+    skip_hbm,
     x_hbm,
     z_hbm,
     b_hbm,
@@ -91,6 +92,8 @@
     gx_ref,
     gg_ref,
     gs_ref,
+    length_ref,
+    skip_ref,
     x_ref,
     z_ref,
     b_ref,
@@ -130,7 +133,7 @@
     sem_shift,
 ):
     length, width = x_ref.shape
-    heads = dt_ref.shape[1]
+    heads = dt_ref.shape[0]
     head_dim = width // heads
     pairs = heads // 2
     lanes = 2 * head_dim
@@ -141,6 +144,7 @@
     loads = {}
     for slot, (name, source, target) in enumerate(
         (
+            ("length", length_hbm, length_ref),
             ("ld", ld_hbm, ld_ref),
             ("dt", dt_hbm, dt_ref),
             ("x", x_hbm, x_ref),
@@ -149,6 +153,7 @@
             ("c", c_hbm, c_ref),
             ("z", z_hbm, z_ref),
             ("gain", gain_hbm, gain_ref),
+            ("skip", skip_hbm, skip_ref),
             ("w", w_hbm, w_ref),
         )
     ):
@@ -196,6 +201,7 @@
     decay_sends = [shift_x(4, 1, row_decay, decay_in.at[0]), shift_x(5, -1, row_decay, decay_in.at[1])]
 
     base = (me_x * ny + me_y) * length
+    loads["length"].wait()
     first = length_ref[0, 0]
     second = first + length_ref[0, 1]
     third = second + length_ref[0, 2]
@@ -221,8 +227,9 @@
 
     loads["ld"].wait()
     loads["dt"].wait()
-    dt = dt_ref[...]
-    running = dot(not_later, ld_ref[...], precision=HIGH)
+    dt_t = dt_ref[...]
+    dt = dot((at_row == at_col).astype(F32), dt_t, 1, 1, precision=HIGH)
+    running = dot(not_later, ld_ref[...], 1, 1, precision=HIGH)
     running_end = running[length - 1 :, :]
     carry_weight = jnp.where(count_heads == 0, jnp.exp(running), 0.0)
     tail_weight = jnp.where(count_heads == count_end, jnp.exp(running_end - running), 0.0)
@@ -247,8 +254,7 @@
     loads["dout"].wait()
     dout_send.start()
 
-    running_t = dot(ld_ref[...], not_later, 0, 1, precision=HIGH)
-    dt_t = dot(dt, (at_row == at_col).astype(F32), 0, 0, precision=HIGH)
+    running_t = dot(ld_ref[...], not_later, 1, 1, precision=HIGH)
     loads["c"].wait()
     c = c_ref[...]
     same_game = count_row == count_col
@@ -277,8 +283,9 @@
     inside = jnp.concatenate(inside, axis=1)
     head_of = lax.broadcasted_iota(jnp.int32, (1, width), 1) // head_dim
     skip = jnp.zeros((1, width), F32)
+    loads["skip"].wait()
     for h in range(heads):
-        skip = jnp.where(head_of == h, skip_ref[h], skip)
+        skip = jnp.where(head_of == h, skip_ref[0, h], skip)
     inside = inside + skip * x
     loads["z"].wait()
     gate = z_ref[...].astype(F32)
@@ -426,7 +433,7 @@
     sums_d_send.receive_all()
     sums = sums_d[0] + sums_d[1]
     gg_ref[...] = sums[:, :width]
-    gs_ref[...] = sums[:, width:]
+    gs_ref[...] = sums[:, width : width + heads]
 
     adj_back_send.receive_all()
     right = dot(b, adj_back_in[...].reshape(ny * rows, width))
@@ -449,6 +456,15 @@
         *decay_sends,
     ):
         sent.finish()
+
+
+def store(*refs):
+    sources, targets, sems = refs[:4], refs[4:8], refs[8]
+    copies = [pltpu.make_async_copy(sources[k], targets[k], sems.at[k]) for k in range(4)]
+    for copy in copies:
+        copy.start()
+    for copy in copies:
+        copy.wait()
 
 
 def mixer(
@@ -480,23 +496,25 @@
     smem = pl.BlockSpec(memory_space=pltpu.SMEM)
     vmem = pl.BlockSpec(memory_space=pltpu.VMEM)
     dma = pltpu.SemaphoreType.DMA
-    out, grad_x, gain_sum, skip_sum = pl.pallas_call(
+    results = pl.pallas_call(
         body,
         out_shape=(
             jax.ShapeDtypeStruct((length, share), BF16),
             jax.ShapeDtypeStruct((length, width), BF16),
             jax.ShapeDtypeStruct((1, width), F32),
-            jax.ShapeDtypeStruct((1, length), F32),
+            jax.ShapeDtypeStruct((1, heads), F32),
         ),
-        in_specs=[smem, smem] + [hbm] * 9,
+        in_specs=[hbm] * 11,
         out_specs=(vmem, vmem, vmem, vmem),
         scratch_shapes=[
+            pltpu.SMEM(game_lengths.shape, jnp.int32),
+            pltpu.SMEM((1, heads), F32),
             pltpu.VMEM((length, width), BF16),
             pltpu.VMEM((length, width), BF16),
             pltpu.VMEM((length, state_dim), BF16),
             pltpu.VMEM((length, state_dim), BF16),
-            pltpu.VMEM((length, heads), F32),
-            pltpu.VMEM((length, heads), F32),
+            pltpu.VMEM((heads, length), F32),
+            pltpu.VMEM((heads, length), F32),
             pltpu.VMEM((1, width), F32),
             pltpu.VMEM(w_out.shape, BF16),
             pltpu.VMEM((nz, length, share), BF16),
@@ -522,7 +540,7 @@
             pltpu.VMEM((ny, 1, pack), F32),
             pltpu.VMEM((nx, 1, pack), F32),
             pltpu.VMEM((nd, 1, pack), F32),
-            dma((9,)),
+            dma((11,)),
             dma((2, 6, ny)),
             dma((2, 3, nz)),
             dma((2, nx)),
@@ -530,23 +548,37 @@
             dma((2, 6)),
         ],
         compiler_params=pltpu.CompilerParams(
-            collective_id=0, has_side_effects=True, vmem_limit_bytes=48 * 1024 * 1024
+            collective_id=0, has_side_effects=True, vmem_limit_bytes=VMEM_LIMIT
         ),
         name="mixer",
     )(
-        game_lengths,
-        skip_d,
-        ssm_input[0],
-        gate_z[0],
-        b_proj[0],
-        c_proj[0],
-        step_size[0],
-        log_decay[0],
-        norm_gain[None],
-        w_out,
-        d_out[0],
+        *(
+            pltpu.with_memory_space_constraint(array, pltpu.HBM)
+            for array in (
+                game_lengths,
+                skip_d[None],
+                ssm_input[0],
+                gate_z[0],
+                b_proj[0],
+                c_proj[0],
+                step_size[0].T,
+                log_decay[0].T,
+                norm_gain[None],
+                w_out,
+                d_out[0],
+            )
+        )
     )
-    return (out[None], grad_x[None], gain_sum[0], skip_sum[0, :heads])
+    out, grad_x, gain_sum, skip_sum = pl.pallas_call(
+        store,
+        out_shape=[jax.ShapeDtypeStruct(r.shape, r.dtype) for r in results],
+        in_specs=[vmem] * 4,
+        out_specs=[hbm] * 4,
+        scratch_shapes=[dma((4,))],
+        compiler_params=pltpu.CompilerParams(vmem_limit_bytes=1 << 20),
+        name="store",
+    )(*results)
+    return (out[None], grad_x[None], gain_sum[0], skip_sum[0])
 
 
 def solution(mesh):

time: 66.1 us -> 53.3 us (0.81)
  local copies, waits for them, and re-layouts: 11.7 us -> 0 us
  Pallas kernels: 53.3 us -> 52.6 us
    unnamed x23 -> x0, local copies, waits for them, and re-layouts: 11.2 us -> none
    pallas_call x1, Pallas kernels: 53.3 us -> 51.8 us  [mixer(): pl.pallas_call(body, out_shape=(jax.ShapeDtypeStruct((length, share), BF1...]
    pallas_call x0 -> x1, Pallas kernels: none -> 0.72 us  [mixer(): pl.pallas_call(store, out_shape=[jax.ShapeDtypeStruct(r.shape, r.dtype) f...]
where the time goes in v2:
time: 53.3 us; the launch traced here: 53.2 us
  Pallas kernels  52.6 us (99%)
  between operations  0.64 us (1%)
    pallas_call x1, Pallas kernels, mixer(): pl.pallas_call(body, out_shape=(jax.ShapeDtypeStruct((length, share), BF1...  51.8 us

profile of v2, /device:TPU:6, one launch (start us, length us, event | category | flops | bytes accessed | tf_op | source)
XLA Modules:
  0.0 53.2 jit_solution(7180249490535661709)
XLA Ops:
  0.6 51.8 %mixer.1 = (bf16[128,256]{1,0:T(8,128)(2,1)S(1)}, bf16[128,512]{1,0:T(8,128)(2,1)S(1)}, f32[1,512]{1,0:T(1,128)S(1)}, f32[1,8]{1,0:T(1,128)S(1)}) custom-call(s32[1,4]{1,0:T(1,128)} %refs_0_.1, f32[1,8]{1,0:T(1,128)} %bitcast.25, bf16[128,512]{1,0:T(8,128)(2,1)} %bitcast.17, bf16[128,512]{1,0:T(8,128)(2,1)} %bitcast.18, bf16[128,128]{1,0:T(8,128)(2,1)} %bitcast.20, ...), custom_call_target="tpu_custom_call" | custom-call | tf_op jit(solution)/shard_map/mixer/pallas_call | solution.py:499
  52.5 0.7 %store.1 = (bf16[128,256]{1,0:T(8,128)(2,1)}, bf16[128,512]{1,0:T(8,128)(2,1)}, f32[1,512]{1,0:T(1,128)}, f32[1,8]{1,0:T(1,128)}) custom-call(bf16[128,256]{1,0:T(8,128)(2,1)S(1)} %get-tuple-element.12.refs_0_, bf16[128,512]{1,0:T(8,128)(2,1)S(1)} %get-tuple-element.13.refs_1_, f32[1,512]{1,0:T(1,128)S(1)} %get-tuple-element.14.refs_2_, ...), custom_call_target="tpu_custom_call" | custom-call | tf_op jit(solution)/shard_map/store/pallas_call | solution.py:572

commit v3 on v2

--- a/solution.py
+++ b/solution.py
@@ -21,37 +21,47 @@
     )
 
 
+def by_distance(size):
+    return sorted(range(1, size), key=lambda k: (-min(k, size - k), k))
+
+
 class Exchange:
     def __init__(self, axis, size, source, landing, sends, receives):
         self.axis, self.size, self.me = axis, size, lax.axis_index(axis)
         self.source, self.landing = source, landing
         self.sends, self.receives = sends, receives
 
-    def copy(self, k, slot):
+    def copy(self, k):
         peer = lax.rem(self.me + k, self.size)
         return pltpu.make_async_remote_copy(
             src_ref=self.source(peer),
-            dst_ref=self.landing.at[slot(peer)],
-            send_sem=self.sends.at[k - 1],
-            recv_sem=self.receives.at[slot(peer)],
+            dst_ref=self.landing.at[self.me],
+            send_sem=self.sends,
+            recv_sem=self.receives,
             device_id={self.axis: peer},
             device_id_type=MESH,
         )
 
     def start(self):
-        for k in range(1, self.size):
-            self.copy(k, lambda peer: self.me).start()
-
-    def receive(self, k):
-        self.copy(k, lambda peer: peer).wait_recv()
+        for k in by_distance(self.size):
+            self.copy(k).start()
+
+    def whole(self):
+        most = self.landing.at[pl.ds(0, self.size - 1)]
+        return pltpu.make_async_remote_copy(
+            src_ref=most,
+            dst_ref=most,
+            send_sem=self.sends,
+            recv_sem=self.receives,
+            device_id={self.axis: lax.rem(self.me + 1, self.size)},
+            device_id_type=MESH,
+        )
 
     def receive_all(self):
-        for k in range(1, self.size):
-            self.receive(k)
+        self.whole().wait_recv()
 
     def finish(self):
-        for k in range(1, self.size):
-            self.copy(k, lambda peer: self.me).wait_send()
+        self.whole().wait_send()
 
 
 class Shift:
@@ -131,6 +141,8 @@
     sem_x,
     sem_d,
     sem_shift,
+    sem_dout,
+    sems_dout,
 ):
     length, width = x_ref.shape
     heads = dt_ref.shape[0]
@@ -140,6 +152,18 @@
     rows = state_in.shape[1]
     total = width * nz
     me_x, me_y, me_z, me_d = (lax.axis_index(a) for a in ("seq_0", "seq_1", "chan", "dp"))
+
+    barrier = pltpu.get_barrier_semaphore()
+    for axis, size, me in (
+        ("seq_1", ny, me_y),
+        ("chan", nz, me_z),
+        ("seq_0", nx, me_x),
+        ("dp", nd, me_d),
+    ):
+        for k in range(1, size):
+            pl.semaphore_signal(
+                barrier, inc=1, device_id={axis: lax.rem(me + k, size)}, device_id_type=MESH
+            )
 
     loads = {}
     for slot, (name, source, target) in enumerate(
@@ -160,18 +184,6 @@
         loads[name] = pltpu.make_async_copy(source, target, load_sem.at[slot])
         loads[name].start()
 
-    barrier = pltpu.get_barrier_semaphore()
-    for axis, size, me in (
-        ("seq_1", ny, me_y),
-        ("chan", nz, me_z),
-        ("seq_0", nx, me_x),
-        ("dp", nd, me_d),
-    ):
-        for k in range(1, size):
-            pl.semaphore_signal(
-                barrier, inc=1, device_id={axis: lax.rem(me + k, size)}, device_id_type=MESH
-            )
-
     def over_y(index, source, landing):
         return Exchange("seq_1", ny, source, landing, sem_y.at[0, index], sem_y.at[1, index])
 
@@ -189,9 +201,32 @@
     adj_send = over_y(3, lambda peer: adj_out.at[peer], adj_in)
     adj_back_send = over_y(4, lambda peer: adj_back_out.at[peer], adj_back_in)
     sums_y_send = over_y(5, lambda peer: sums_y.at[me_y], sums_y)
-    dout_send = over_z(0, lambda peer: dout_all.at[me_z], dout_all)
-    stat_send = over_z(1, lambda peer: stat_all.at[me_z], stat_all)
-    proj_send = over_z(2, lambda peer: proj_out.at[peer], proj_in)
+
+    def around(step):
+        return lax.rem(me_z + nz + step, nz)
+
+    def dout_copy(source, step, sem, half=None):
+        piece = dout_all.at[source]
+        if half is not None:
+            piece = dout_all.at[source, pl.ds(half * (length // 2), length // 2)]
+        return pltpu.make_async_remote_copy(
+            src_ref=piece,
+            dst_ref=piece,
+            send_sem=sem_dout,
+            recv_sem=sems_dout.at[sem],
+            device_id={"chan": around(step)},
+            device_id_type=MESH,
+        )
+
+    dout_sends = [dout_copy(me_z, step, me_z) for step in (2, -2, 1, -1)]
+    dout_forwards = [
+        dout_copy(around(-2), 2, around(-2), half=0),
+        dout_copy(around(2), -2, nz, half=1),
+        dout_copy(around(-2), 1, around(-2)),
+        dout_copy(around(2), -1, around(2)),
+    ]
+    stat_send = over_z(0, lambda peer: stat_all.at[me_z], stat_all)
+    proj_send = over_z(1, lambda peer: proj_out.at[peer], proj_in)
     sums_x_send = Exchange(
         "seq_0", nx, lambda peer: sums_x.at[me_x], sums_x, sem_x.at[0], sem_x.at[1]
     )
@@ -252,7 +287,8 @@
     decay_send.start()
     state_send.start()
     loads["dout"].wait()
-    dout_send.start()
+    for send in dout_sends:
+        send.start()
 
     running_t = dot(ld_ref[...], not_later, 1, 1, precision=HIGH)
     loads["c"].wait()
@@ -305,9 +341,27 @@
     row_state[...] = state.astype(BF16)
     for shift in row_sends:
         shift.start()
+    for step in (-2, 2):
+        dout_copy(around(step), step, around(step)).wait_recv()
+    for forward in dout_forwards:
+        forward.start()
+    for step in (-1, 1):
+        dout_copy(around(step), step, around(step)).wait_recv()
     loads["w"].wait()
     loads["gain"].wait()
     gain = gain_ref[...]
+    share = dout_all.shape[2]
+
+    def columns(peer):
+        return pl.ds(pl.multiple_of(peer * share, share), share)
+
+    def pulled_from(step):
+        peer = around(step)
+        return dot(dout_all[peer], w_ref[:, columns(peer)], 1, 1)
+
+    pulled = pulled_from(0)
+    for step in (-1, 1, -2, 2):
+        pulled = pulled + pulled_from(step)
     for shift in decay_sends:
         shift.receive()
     for shift in row_sends:
@@ -322,16 +376,12 @@
     back_in[me_y] = back_out[me_y]
     back_send.start()
 
-    share = dout_all.shape[2]
-
-    def columns(peer):
-        return pl.ds(pl.multiple_of(peer * share, share), share)
-
-    pulled = dot(dout_all[me_z], w_ref[:, columns(me_z)], 1, 1)
-    for k in range(1, nz):
-        dout_send.receive(k)
-        peer = lax.rem(me_z + k, nz)
-        pulled = pulled + dot(dout_all[peer], w_ref[:, columns(peer)], 1, 1)
+    for step in (-3, 3):
+        dout_copy(around(step), step, around(step)).wait_recv()
+        pulled = pulled + pulled_from(step)
+    dout_copy(around(4), 4, around(4), half=0).wait_recv()
+    dout_copy(around(4), 4, nz, half=1).wait_recv()
+    pulled = pulled + pulled_from(4)
 
     back_send.receive_all()
     from_left = dot(c, back_in[...].reshape(ny * rows, width))
@@ -348,10 +398,10 @@
         [over_features(gated * gated), over_features(normed.astype(F32) * pulled)], axis=0
     )
     stat_send.start()
-    for k in range(1, nz):
+    for k in by_distance(nz):
         peer = lax.rem(me_z + k, nz)
         proj_out[peer] = dot(normed, w_ref[:, columns(peer)]).astype(BF16)
-        proj_send.copy(k, lambda peer: me_z).start()
+        proj_send.copy(k).start()
     projected = dot(normed, w_ref[:, columns(me_z)])
     stat_send.receive_all()
     stats = stat_all[0]
@@ -398,13 +448,6 @@
     adj_row[...] = later.astype(BF16)
     for shift in adj_row_sends:
         shift.start()
-
-    sums_y_send.receive_all()
-    sums = sums_y[0]
-    for k in range(1, ny):
-        sums = sums + sums_y[k]
-    sums_x[me_x] = sums
-    sums_x_send.start()
 
     for shift in adj_row_sends:
         shift.receive()
@@ -418,6 +461,13 @@
     adj_back_in[me_y] = adj_back_out[me_y]
     adj_back_send.start()
 
+    sums_y_send.receive_all()
+    sums = sums_y[0]
+    for k in range(1, ny):
+        sums = sums + sums_y[k]
+    sums_x[me_x] = sums
+    sums_x_send.start()
+
     sums_x_send.receive_all()
     sums = sums_x[0]
     for k in range(1, nx):
@@ -425,8 +475,8 @@
     sums_d[me_d] = sums
     sums_d_send.start()
 
+    proj_send.receive_all()
     for k in range(1, nz):
-        proj_send.receive(k)
         projected = projected + proj_in[lax.rem(me_z + k, nz)].astype(F32)
     out_ref[...] = (jnp.concatenate([inv] * (share // length), axis=1) * projected).astype(BF16)
 
@@ -446,7 +496,6 @@
         adj_send,
         adj_back_send,
         sums_y_send,
-        dout_send,
         stat_send,
         proj_send,
         sums_x_send,
@@ -456,6 +505,8 @@
         *decay_sends,
     ):
         sent.finish()
+    for sent in (*dout_sends, *dout_forwards):
+        sent.wait_send()
 
 
 def store(*refs):
@@ -541,11 +592,13 @@
             pltpu.VMEM((nx, 1, pack), F32),
             pltpu.VMEM((nd, 1, pack), F32),
             dma((11,)),
-            dma((2, 6, ny)),
-            dma((2, 3, nz)),
-            dma((2, nx)),
-            dma((2, nd)),
             dma((2, 6)),
+            dma((2, 2)),
+            dma((2,)),
+            dma((2,)),
+            dma((2, 6)),
+            dma(()),
+            dma((nz + 1,)),
         ],
         compiler_params=pltpu.CompilerParams(
             collective_id=0, has_side_effects=True, vmem_limit_bytes=VMEM_LIMIT

time: 53.3 us -> 51.4 us (0.964)
  the two profiles are of different devices: /device:TPU:6 before, /device:TPU:1 now
where the time goes in v3:
time: 51.4 us; the launch traced here: 51.3 us
  Pallas kernels  50.7 us (99%)
  between operations  0.64 us (1%)
    pallas_call x1, Pallas kernels, mixer(): pl.pallas_call(body, out_shape=(jax.ShapeDtypeStruct((length, share), BF1...  49.9 us

profile of v3, /device:TPU:1, one launch (start us, length us, event | category | flops | bytes accessed | tf_op | source)
XLA Modules:
  0.0 51.3 jit_solution(5804226760305292813)
XLA Ops:
  0.6 49.9 %mixer.1 = (bf16[128,256]{1,0:T(8,128)(2,1)S(1)}, bf16[128,512]{1,0:T(8,128)(2,1)S(1)}, f32[1,512]{1,0:T(1,128)S(1)}, f32[1,8]{1,0:T(1,128)S(1)}) custom-call(s32[1,4]{1,0:T(1,128)} %refs_0_.1, f32[1,8]{1,0:T(1,128)} %bitcast.25, bf16[128,512]{1,0:T(8,128)(2,1)} %bitcast.17, bf16[128,512]{1,0:T(8,128)(2,1)} %bitcast.18, bf16[128,128]{1,0:T(8,128)(2,1)} %bitcast.20, ...), custom_call_target="tpu_custom_call" | custom-call | tf_op jit(solution)/shard_map/mixer/pallas_call | solution.py:550
  50.6 0.7 %store.1 = (bf16[128,256]{1,0:T(8,128)(2,1)}, bf16[128,512]{1,0:T(8,128)(2,1)}, f32[1,512]{1,0:T(1,128)}, f32[1,8]{1,0:T(1,128)}) custom-call(bf16[128,256]{1,0:T(8,128)(2,1)S(1)} %get-tuple-element.12.refs_0_, bf16[128,512]{1,0:T(8,128)(2,1)S(1)} %get-tuple-element.13.refs_1_, f32[1,512]{1,0:T(1,128)S(1)} %get-tuple-element.14.refs_2_, ...), custom_call_target="tpu_custom_call" | custom-call | tf_op jit(solution)/shard_map/store/pallas_call | solution.py:625
